TPU v7x, 32 devices: a whole 2x2x4 slice. The times are simulated.
32 devices in a mesh: grp: 2 (over y), tgt: 4 (over z), src: 4 (over x, core).
Axes of the slice: x: 2, y: 2, z: 4, core: 2. Of those that a mesh axis runs over, the one named last changes fastest.
Arguments:
- target_rows: bfloat16 [2048, 4608], P(('grp', 'tgt', 'src')), parts along dimension 0, may hold values from -6 to 6
- target_pos: int32 [2048], P(('grp', 'tgt')), parts along dimension 0, may hold values from 0 to 255
- decoder_rows: bfloat16 [512, 4608], P(('grp', 'tgt', 'src')), parts along dimension 0, may hold values from -0.09375 to 0.09375
- source_pos: int32 [512], P('grp'), parts along dimension 0, may hold values from 0 to 255
- out_proj: bfloat16 [32, 4608, 128], P('src', 'tgt'), may hold values from -0.09375 to 0.09375
- value_proj: bfloat16 [16, 4608, 128], P('src'), may hold values from -1 to 1
- attention: bfloat16 [64, 256, 256], P(('grp', 'src'), 'tgt'), parts along dimension 0, may hold values from 0 to 1, as said below
- tile_pattern: int32 [8, 4], P('grp'), parts along dimension 0, may hold values from 0 to 1, as said below
Outputs:
- edges: bfloat16 [512, 1024], P(('grp', 'src'), 'tgt'), parts along dimension 0
There are 2 independent parts, one for each index of `grp`. A program takes and returns all parts, laid end to end along the dimension named above; an argument that names none is the same for every part. Nothing has to cross between parts.
Inputs may be any that keep to these rules, and one draw needn't show every extreme that they name: Each row attention[h, p, :] is a probability distribution over the keys 0 to p: zero beyond p, summing to one. tile_pattern[b, c] is 1 where the tile of edges between source block b and target block c is kept, else 0.
All inputs are finite; a program needn't handle non-finite values.
Results may differ from a plain program's by a relative error of at most 0.0057.
Values may be sent and summed in bfloat16 or wider, within the bound.
A program may use at most 64 MiB of HBM per device.

v0:
```python
import jax
import jax.numpy as jnp
from jax import lax
from jax.sharding import PartitionSpec as P


def passed_along(value, axis, steps):
    count = lax.axis_size(axis)
    pairs = [(source, (source + steps) % count) for source in range(count)]
    return lax.ppermute(value, axis, pairs)


def shards(
    target_rows, target_pos, decoder_rows, source_pos, out_proj, value_proj, attention, tile_pattern
):
    blocks = lax.axis_size("tgt")
    column = lax.axis_index("tgt")
    src_lane = lax.axis_index("src")
    full_targets, full_sources = (
        lax.all_gather(target_rows, "src", axis=0, tiled=True),
        lax.all_gather(decoder_rows, "src", axis=0, tiled=True),
    )
    tgt_dev = full_targets.shape[0]
    src_dev = full_sources.shape[0]
    sub_rows = decoder_rows.shape[0]
    heads_here = out_proj.shape[0]
    head_dim = out_proj.shape[2]
    groups_here = value_proj.shape[0]
    repeat = heads_here // groups_here
    read_sum = jnp.einsum(
        "td,hde->the",
        full_targets,
        lax.all_gather(out_proj, "tgt", axis=1, tiled=True),
        preferred_element_type=jnp.float32,
    )
    head_reads = read_sum.astype(jnp.bfloat16).reshape(tgt_dev, groups_here, repeat, head_dim)
    values = jnp.einsum("sd,gde->sge", full_sources, value_proj, preferred_element_type=jnp.float32)
    values = values.astype(jnp.bfloat16).reshape(src_dev, groups_here * head_dim)
    attn_table = lax.all_gather(attention, "tgt", axis=1, tiled=True)
    target_attn = jnp.take(attn_table, target_pos, axis=1)
    keyed_attn = jnp.transpose(target_attn, (0, 2, 1))

    def edge_tile(payload, block_index):
        decoder_part, value_part = payload
        key_positions = lax.dynamic_slice_in_dim(source_pos, block_index * src_dev, src_dev)
        weights = jnp.take(keyed_attn, key_positions, axis=1).astype(jnp.float32)
        scores = jnp.einsum(
            "sgd,tgrd->grst",
            value_part.reshape(src_dev, groups_here, head_dim),
            head_reads,
            preferred_element_type=jnp.float32,
        )
        scores = scores.reshape(heads_here, src_dev, tgt_dev)
        mixed_term = jnp.sum(weights * scores, axis=0)
        own_positions = lax.dynamic_slice_in_dim(key_positions, src_lane * sub_rows, sub_rows)
        same_place = (own_positions[:, None] == target_pos[None, :]).astype(jnp.float32)
        direct = (
            jnp.einsum("sd,td->st", decoder_part, full_targets, preferred_element_type=jnp.float32)
            * same_place
        )
        own_rows = lax.dynamic_slice_in_dim(mixed_term, src_lane * sub_rows, sub_rows, 0)
        return lax.dynamic_update_slice_in_dim(
            mixed_term, own_rows + direct, src_lane * sub_rows, 0
        )

    def place_tile(partial_value, payload, block_index):
        kept_flag = tile_pattern[block_index, column]
        piece_tile = edge_tile(payload, block_index) * kept_flag.astype(jnp.float32)
        return lax.dynamic_update_slice_in_dim(partial_value, piece_tile, block_index * src_dev, 0)

    own_block = (decoder_rows, values)
    partial_value = jnp.zeros((blocks * src_dev, tgt_dev), jnp.float32)
    partial_value = place_tile(partial_value, own_block, column)

    def cycle_turn(turn_index, state_carry):
        forward_block, backward_block, running = state_carry
        forward_block = passed_along((forward_block[0], forward_block[1]), "tgt", 1)
        backward_block = passed_along((backward_block[0], backward_block[1]), "tgt", -1)
        running = place_tile(running, forward_block, (column - turn_index) % blocks)
        running = place_tile(running, backward_block, (column + turn_index) % blocks)
        return (forward_block, backward_block, running)

    forward_block, backward_block, partial_value = lax.fori_loop(
        1, blocks // 2, cycle_turn, (own_block, own_block, partial_value)
    )
    forward_block = passed_along((forward_block[0], forward_block[1]), "tgt", 1)
    partial_value = place_tile(partial_value, forward_block, (column - blocks // 2) % blocks)
    summed = lax.psum_scatter(partial_value, "src", scatter_dimension=0, tiled=True)
    return summed.astype(jnp.bfloat16)


def solution(mesh):
    return jax.shard_map(
        shards,
        mesh=mesh,
        in_specs=(
            P(("grp", "tgt", "src"), None),
            P(("grp", "tgt")),
            P(("grp", "tgt", "src"), None),
            P("grp"),
            P("src", "tgt", None),
            P("src", None, None),
            P(("grp", "src"), "tgt", None),
            P("grp", None),
        ),
        out_specs=P(("grp", "src"), "tgt"),
        check_vma=False,
    )
```

profile of v0, /device:TPU:0, one launch (start us, length us, event | category | flops | bytes accessed | tf_op | source)
XLA Modules:
  0.0 277.3 jit_solution(18094460157816442848)
XLA Ops:
  6.5 1.9 copy.26
  8.5 0.7 all-gather.6.cloned.1.call-update
  9.2 0.7 all-gather.8.cloned.1.call-update
  10.0 5.1 %collective-permute-start.3 = (bf16[16,4608]{1,0:T(8,128)(2,1)S(1)}, bf16[16,4608]{1,0:T(8,128)(2,1)S(1)}, u32[]{:S(2)}, u32[]{:S(2)}) collective-permute-start(bf16[16,4608]{1,0:T(8,128)(2,1)S(1)} %copy-done.2), channel_id=1, source_target_pairs={{0,12},{4,0},{8,4},{12,8},{1,13},{5,1},{9,5},{13,9},{2,14},{6,2},{... | collective-permute-start | bytes 442376 | tf_op jit(solution)/shard_map/while/body/eval_jaxpr/ppermute | solution.py:10
  15.1 7.5 %all_gather.15 = bf16[64,4608]{1,0:T(8,128)(2,1)S(1)} all-gather(bf16[16,4608]{1,0:T(8,128)(2,1)S(1)} %copy-done.2), channel_id=1, replica_groups=mesh['grp'=2,'tgt'=4,'src'=4] {'src'}, dimensions={0}, use_global_device_ids=true | all-gather | bytes 737280 | tf_op jit(solution)/shard_map/all_gather | solution.py:21
  22.6 3.3 %convolution_convert_fusion = bf16[64,4,128]{2,0,1:T(8,128)(2,1)S(1)} fusion(bf16[4,4608,128]{2,1,0:T(8,128)(2,1)} %param.15, bf16[64,4608]{1,0:T(8,128)(2,1)S(1)} %all_gather.15), kind=kOutput, calls=%fused_computation.8 | convolution fusion | flops 302022656 | bytes 5373952 | tf_op jit(solution)/shard_map/sd,gde->sge/dot_general | solution.py:37
  26.0 3.9 %collective-permute-start.2 = (bf16[64,512]{1,0:T(8,128)(2,1)S(1)}, bf16[64,512]{1,0:T(8,128)(2,1)S(1)}, u32[]{:S(2)}, u32[]{:S(2)}) collective-permute-start(bf16[64,512]{1,0:T(8,128)(2,1)S(1)} %copy_bitcast_fusion), channel_id=1, source_target_pairs={{0,12},{4,0},{8,4},{12,8},{1,13},{5,1},{9,5},{13,9},{2,14},{6,2},{... | collective-permute-start | bytes 196616 | tf_op jit(solution)/shard_map/while/body/eval_jaxpr/ppermute | solution.py:10
  30.1 0.7 fusion.26
  33.4 4.4 %collective-permute-done = bf16[64,512]{1,0:T(8,128)(2,1)S(1)} collective-permute-done((bf16[64,512]{1,0:T(8,128)(2,1)S(1)}, bf16[64,512]{1,0:T(8,128)(2,1)S(1)}, u32[]{:S(2)}, u32[]{:S(2)}) %collective-permute-start) | collective-permute-done | bytes 65568 | tf_op jit(solution)/shard_map/while/body/eval_jaxpr/ppermute | solution.py:10
  37.8 1.1 collective-permute-start.4
  39.0 5.8 %collective-permute-done.4 = bf16[64,512]{1,0:T(8,128)(2,1)S(1)} collective-permute-done((bf16[64,512]{1,0:T(8,128)(2,1)S(1)}, bf16[64,512]{1,0:T(8,128)(2,1)S(1)}, u32[]{:S(2)}, u32[]{:S(2)}) %collective-permute-start.4) | collective-permute-done | bytes 65568 | tf_op jit(solution)/shard_map/ppermute | solution.py:10
  44.9 2.0 gather_fusion
  46.9 0.9 select_bitcast_fusion
  47.8 1.3 copy.27
  49.1 0.6 gather_fusion.4
  49.7 0.6 gather_fusion.3
  50.3 0.6 gather_fusion.2
  50.9 0.6 gather_fusion.1
  51.5 17.4 %all-gather.6.cloned.1.call-done = bf16[256,4608]{1,0:T(8,128)(2,1)} async-done(((bf16[64,4608]{1,0:T(8,128)(2,1)}), bf16[256,4608]{1,0:T(8,128)(2,1)}) %all-gather.6.cloned.1.call-update) | async-done | bytes 2359312 | tf_op jit(solution)/shard_map/all_gather | solution.py:20
  68.9 168.4 %all-gather.8.cloned.1.call-done = bf16[8,4608,128]{2,1,0:T(8,128)(2,1)} async-done(((bf16[8,1152,128]{2,1,0:T(8,128)(2,1)}), bf16[8,4608,128]{2,1,0:T(8,128)(2,1)}) %all-gather.8.cloned.1.call-update) | async-done | bytes 9437200 | tf_op jit(solution)/shard_map/all_gather | solution.py:33
  237.2 7.0 %fusion.2 = bf16[256,8,128]{2,0,1:T(8,128)(2,1)S(1)} fusion(bf16[8,4608,128]{2,1,0:T(8,128)(2,1)} %all-gather.8.cloned.1.call-done, bf16[256,4608]{1,0:T(8,128)(2,1)} %all-gather.6.cloned.1.call-done), kind=kOutput, calls=%fused_computation.7 | convolution fusion | flops 2416181248 | bytes 12320768 | tf_op jit(solution)/shard_map/td,hde->the/dot_general | solution.py:30
  245.5 0.4 fusion.16
  245.9 0.4 fusion.17
  246.3 0.7 fusion.12
  247.1 0.7 fusion.10
  247.9 0.4 fusion.15
  248.3 0.7 fusion.8
  249.1 0.4 fusion.14
  249.5 0.7 fusion.6
  250.3 0.7 copy-done.1
  251.0 18.4 %reduce-scatter.2.cloned.1.call-done = f32[64,256]{1,0:T(8,128)} async-done(((f32[256,256]{1,0:T(8,128)}), f32[64,256]{1,0:T(8,128)}) %reduce-scatter.2.cloned.1.call-update) | async-done | bytes 65552 | tf_op jit(solution)/shard_map/reduce_scatter | solution.py:88
  269.3 1.5 convert_element_type.69
  (46 shorter events, 1.9 us)
Async XLA Ops:
  6.5 3.4 %copy-start.2 = (bf16[16,4608]{1,0:T(8,128)(2,1)S(1)}, bf16[16,4608]{1,0:T(8,128)(2,1)}, u32[]{:S(2)}) copy-start(bf16[16,4608]{1,0:T(8,128)(2,1)} %param.12) | copy-start | bytes 442372
  6.5 38.4 %all-gather.4.cloned.1.call-start = ((), (), s32[]{:S(2)}) async-start(), calls=%async_computation.1 | async-start | bytes 1310720 | tf_op jit(solution)/shard_map/all_gather | solution.py:39
  8.4 60.4 %all-gather.6.cloned.1.call-start = ((), (), s32[]{:S(2)}) async-start(), calls=%async_computation.2 | async-start | bytes 2949120 | tf_op jit(solution)/shard_map/all_gather | solution.py:20
  9.2 228.1 %all-gather.8.cloned.1.call-start = ((), (), s32[]{:S(2)}) async-start(), calls=%async_computation.3 | async-start | bytes 11796480 | tf_op jit(solution)/shard_map/all_gather | solution.py:33
  9.9 259.4 %reduce-scatter.2.cloned.1.call-start = ((), (), s32[]{:S(2)}) async-start(), calls=%async_computation.4 | async-start | bytes 327680 | tf_op jit(solution)/shard_map/reduce_scatter | solution.py:88
  10.0 238.3 %collective-permute-start.3 = (bf16[16,4608]{1,0:T(8,128)(2,1)S(1)}, bf16[16,4608]{1,0:T(8,128)(2,1)S(1)}, u32[]{:S(2)}, u32[]{:S(2)}) collective-permute-start(bf16[16,4608]{1,0:T(8,128)(2,1)S(1)} %copy-done.2), channel_id=1, source_target_pairs={{0,12},{4,0},{8,4},{12,8},{1,13},{5,1},{9,5},{13,9},{2,14},{6,2},{... | collective-permute-start | bytes 442376 | tf_op jit(solution)/shard_map/while/body/eval_jaxpr/ppermute | solution.py:10
  15.1 29.7 %collective-permute-start.1 = (bf16[16,4608]{1,0:T(8,128)(2,1)S(1)}, bf16[16,4608]{1,0:T(8,128)(2,1)S(1)}, u32[]{:S(2)}, u32[]{:S(2)}) collective-permute-start(bf16[16,4608]{1,0:T(8,128)(2,1)S(1)} %copy-done.2), channel_id=1, source_target_pairs={{0,4},{4,8},{8,12},{12,0},{1,5},{5,9},{9,13},{13,1},{2,6},{6,10},{... | collective-permute-start | bytes 442376 | tf_op jit(solution)/shard_map/while/body/eval_jaxpr/ppermute | solution.py:10
  22.6 7.2 %copy-start.3 = (s32[256]{0:T(256)S(1)}, s32[256]{0:T(256)}, u32[]{:S(2)}) copy-start(s32[256]{0:T(256)} %param.11) | copy-start | bytes 3076
  22.6 7.3 %copy-start.4 = (s32[256]{0:T(256)S(1)}, s32[256]{0:T(256)}, u32[]{:S(2)}) copy-start(s32[256]{0:T(256)} %param.13) | copy-start | bytes 3076
  22.6 7.5 %copy-start.5 = (s32[4,4]{1,0:T(4,128)S(1)}, s32[4,4]{1,0:T(4,128)}, u32[]{:S(2)}) copy-start(s32[4,4]{1,0:T(4,128)} %param.17) | copy-start | bytes 196
  26.0 13.0 %collective-permute-start.2 = (bf16[64,512]{1,0:T(8,128)(2,1)S(1)}, bf16[64,512]{1,0:T(8,128)(2,1)S(1)}, u32[]{:S(2)}, u32[]{:S(2)}) collective-permute-start(bf16[64,512]{1,0:T(8,128)(2,1)S(1)} %copy_bitcast_fusion), channel_id=1, source_target_pairs={{0,12},{4,0},{8,4},{12,8},{1,13},{5,1},{9,5},{13,9},{2,14},{6,2},{... | collective-permute-start | bytes 196616 | tf_op jit(solution)/shard_map/while/body/eval_jaxpr/ppermute | solution.py:10
  29.8 7.9 %collective-permute-start = (bf16[64,512]{1,0:T(8,128)(2,1)S(1)}, bf16[64,512]{1,0:T(8,128)(2,1)S(1)}, u32[]{:S(2)}, u32[]{:S(2)}) collective-permute-start(bf16[64,512]{1,0:T(8,128)(2,1)S(1)} %copy_bitcast_fusion), channel_id=1, source_target_pairs={{0,4},{4,8},{8,12},{12,0},{1,5},{5,9},{9,13},{13,1},{2,6},{6,10},{... | collective-permute-start | bytes 196616 | tf_op jit(solution)/shard_map/while/body/eval_jaxpr/ppermute | solution.py:10
  37.8 7.0 %collective-permute-start.4 = (bf16[64,512]{1,0:T(8,128)(2,1)S(1)}, bf16[64,512]{1,0:T(8,128)(2,1)S(1)}, u32[]{:S(2)}, u32[]{:S(2)}) collective-permute-start(bf16[64,512]{1,0:T(8,128)(2,1)S(1)} %collective-permute-done), channel_id=1, source_target_pairs={{0,4},{4,8},{8,12},{12,0},{1,5},{5,9},{9,13},{13,1},{2,6},{6,10},{... | collective-permute-start | bytes 196616 | tf_op jit(solution)/shard_map/ppermute | solution.py:10
  44.8 204.7 %collective-permute-start.5 = (bf16[16,4608]{1,0:T(8,128)(2,1)S(1)}, bf16[16,4608]{1,0:T(8,128)(2,1)S(1)}, u32[]{:S(2)}, u32[]{:S(2)}) collective-permute-start(bf16[16,4608]{1,0:T(8,128)(2,1)S(1)} %collective-permute-done.1), channel_id=1, source_target_pairs={{0,4},{4,8},{8,12},{12,0},{1,5},{5,9},{9,13},{13,1},{2,6},{6,10},{... | collective-permute-start | bytes 442376 | tf_op jit(solution)/shard_map/ppermute | solution.py:10
  244.5 1.8 copy-start
  250.3 0.7 copy-start.1
Sparse Core Ops, SparseCore 0:
  8.9 33.7 all-gather.3
  44.2 24.5 all-gather.5
  70.4 166.7 all-gather.7
  251.1 18.2 reduce-scatter.1
where the time goes:
time: 278 us; the launch traced here: 277 us
  waiting for transfers between devices  216 us (78%)
  between operations  16 us (6%)
  matrix products  14.3 us (5%)
  starting transfers between devices  10.4 us (4%)
  local copies, waits for them, and re-layouts  9.07 us (3%)
  blocking collectives  7.51 us (3%)
  other arithmetic  4.37 us (2%)
    all_gather x1, waiting for transfers between devices, shards(): lax.all_gather(out_proj, 'tgt', axis=1, tiled=True)  168 us
    reduce_scatter x1, waiting for transfers between devices, shards(): lax.psum_scatter(partial_value, 'src', scatter_dimension=0, tiled=True)  18.4 us
    all_gather x1, waiting for transfers between devices, shards(): lax.all_gather(target_rows, 'src', axis=0, tiled=True)  17.4 us
    ppermute x6, starting transfers between devices, passed_along(): return lax.ppermute(value, axis, pairs)  10.2 us
    ppermute x6, waiting for transfers between devices, passed_along(): return lax.ppermute(value, axis, pairs)  10.2 us
    all_gather x1, blocking collectives, shards(): lax.all_gather(decoder_rows, 'src', axis=0, tiled=True)  7.51 us
    dot_general x1, matrix products, shards(): jnp.einsum('td,hde->the', full_targets, lax.all_gather(out_proj, 'tgt', a...  6.99 us
  transfers between devices with their start and end apart: 10, of which 5 were waited for; matrix products, arithmetic and copies ran while one was open for 8% of the time, Pallas kernels for 0%

commit v1 on v0

--- a/solution.py
+++ b/solution.py
@@ -27,12 +27,38 @@
     head_dim = out_proj.shape[2]
     groups_here = value_proj.shape[0]
     repeat = heads_here // groups_here
-    read_sum = jnp.einsum(
+    size, index, rows = (lax.axis_size("tgt"), lax.axis_index("tgt"), out_proj.shape[1])
+    forward = [(i, (i + 1) % size) for i in range(size)]
+    downward = [(i, (i - 1) % size) for i in range(size)]
+    halfway = size // 2
+    from_left = from_right = out_proj
+    total = jnp.einsum(
         "td,hde->the",
-        full_targets,
-        lax.all_gather(out_proj, "tgt", axis=1, tiled=True),
+        lax.dynamic_slice_in_dim(full_targets, index * rows, out_proj.shape[1], axis=1),
+        out_proj,
         preferred_element_type=jnp.float32,
     )
+    for turn in range(1, halfway + 1):
+        from_left = lax.ppermute(from_left, "tgt", forward)
+        if turn < size - halfway:
+            from_right = lax.ppermute(from_right, "tgt", downward)
+            total = total + jnp.einsum(
+                "td,hde->the",
+                lax.dynamic_slice_in_dim(
+                    full_targets, (index + turn) % size * rows, from_right.shape[1], axis=1
+                ),
+                from_right,
+                preferred_element_type=jnp.float32,
+            )
+        total = total + jnp.einsum(
+            "td,hde->the",
+            lax.dynamic_slice_in_dim(
+                full_targets, (index - turn) % size * rows, from_left.shape[1], axis=1
+            ),
+            from_left,
+            preferred_element_type=jnp.float32,
+        )
+    read_sum = total
     head_reads = read_sum.astype(jnp.bfloat16).reshape(tgt_dev, groups_here, repeat, head_dim)
     values = jnp.einsum("sd,gde->sge", full_sources, value_proj, preferred_element_type=jnp.float32)
     values = values.astype(jnp.bfloat16).reshape(src_dev, groups_here * head_dim)

time: 278 us -> 254 us (0.914)
  waiting for transfers between devices: 216 us -> 125 us
  starting transfers between devices: 10.4 us -> 63 us
  local copies, waits for them, and re-layouts: 9.07 us -> 15 us
  matrix products: 14.3 us -> 19.8 us
  other arithmetic: 4.37 us -> 7.33 us
    all_gather x1 -> x0, waiting for transfers between devices: 168 us -> none  [shards(): lax.all_gather(out_proj, 'tgt', axis=1, tiled=True)]
    ppermute x0 -> x3, starting transfers between devices: none -> 55.1 us  [the longest x2 52.4 us: shards(): from_left = lax.ppermute(from_left, 'tgt', forward)]
    ppermute x0 -> x3, waiting for transfers between devices: none -> 53.4 us  [the longest x2 53.4 us: shards(): from_left = lax.ppermute(from_left, 'tgt', forward)]
    ppermute x6, waiting for transfers between devices: 10.2 us -> 48.9 us  [passed_along(): return lax.ppermute(value, axis, pairs)]
    all_gather x1, waiting for transfers between devices: 17.4 us -> 0.01 us  [shards(): lax.all_gather(target_rows, 'src', axis=0, tiled=True)]
    reduce_scatter x1, waiting for transfers between devices: 18.4 us -> 22.4 us  [shards(): lax.psum_scatter(partial_value, 'src', scatter_dimension=0, tiled=True)]
    dot_general x4, matrix products: 2.81 us -> 6.47 us  [edge_tile(): jnp.einsum('sd,td->st', decoder_part, full_targets, preferred_element_typ...]
    gather x4, local copies, waits for them, and re-layouts: 2.38 us -> 5.46 us  [edge_tile(): weights = jnp.take(keyed_attn, key_positions, axis=1).astype(jnp.float32)]
  transfers between devices with their start and end apart: 10 -> 12, of which waited for: 5 -> 4; matrix products, arithmetic and copies ran while one was open for 8% -> 14% of each run, Pallas kernels for 0% -> 0%
where the time goes in v1:
time: 254 us
  waiting for transfers between devices  125 us (49%)
  starting transfers between devices  63 us (25%)
  matrix products  19.8 us (8%)
  between operations  16.1 us (6%)
  local copies, waits for them, and re-layouts  15 us (6%)
  blocking collectives  7.72 us (3%)
  other arithmetic  7.33 us (3%)
    ppermute x2, waiting for transfers between devices, shards(): from_left = lax.ppermute(from_left, 'tgt', forward)  53.4 us
    ppermute x2, starting transfers between devices, shards(): from_left = lax.ppermute(from_left, 'tgt', forward)  52.4 us
    ppermute x6, waiting for transfers between devices, passed_along(): return lax.ppermute(value, axis, pairs)  48.9 us
    reduce_scatter x1, waiting for transfers between devices, shards(): lax.psum_scatter(partial_value, 'src', scatter_dimension=0, tiled=True)  22.4 us
    ppermute x6, starting transfers between devices, passed_along(): return lax.ppermute(value, axis, pairs)  7.84 us
    all_gather x1, blocking collectives, shards(): lax.all_gather(decoder_rows, 'src', axis=0, tiled=True)  7.72 us
    dot_general x4, matrix products, edge_tile(): jnp.einsum('sd,td->st', decoder_part, full_targets, preferred_element_typ...  6.47 us
    gather x4, local copies, waits for them, and re-layouts, edge_tile(): weights = jnp.take(keyed_attn, key_positions, axis=1).astype(jnp.float32)  5.46 us
  transfers between devices with their start and end apart: 12, of which 4 were waited for; matrix products, arithmetic and copies ran while one was open for 14% of the time, Pallas kernels for 0%

profile of v1, /device:TPU:0, one launch (start us, length us, event | category | flops | bytes accessed | tf_op | source)
XLA Modules:
  0.0 253.8 jit_solution(5526496660185962488)
XLA Ops:
  6.5 1.8 copy.26
  8.5 3.1 %collective-permute-start.1 = (bf16[8,1152,128]{2,1,0:T(8,128)(2,1)}, bf16[8,1152,128]{2,1,0:T(8,128)(2,1)S(1)}, u32[]{:S(2)}, u32[]{:S(2)}) collective-permute-start(bf16[8,1152,128]{2,1,0:T(8,128)(2,1)} %param.14), channel_id=1, source_target_pairs={{0,4},{4,8},{8,12},{12,0},{1,5},{5,9},{9,13},{13,1},{2,6},{6,10},{... | collective-permute-start | bytes 7077896 | tf_op jit(solution)/shard_map/ppermute | solution.py:42
  11.6 2.7 %collective-permute-start = (bf16[8,1152,128]{2,1,0:T(8,128)(2,1)}, bf16[8,1152,128]{2,1,0:T(8,128)(2,1)}, u32[]{:S(2)}, u32[]{:S(2)}) collective-permute-start(bf16[8,1152,128]{2,1,0:T(8,128)(2,1)} %param.14), channel_id=1, source_target_pairs={{0,12},{4,0},{8,4},{12,8},{1,13},{5,1},{9,5},{13,9},{2,14},{6,2},{... | collective-permute-start | bytes 7077896 | tf_op jit(solution)/shard_map/ppermute | solution.py:44
  14.3 7.7 %all_gather.11 = bf16[64,4608]{1,0:T(8,128)(2,1)S(1)} all-gather(bf16[16,4608]{1,0:T(8,128)(2,1)} %param.12), channel_id=1, replica_groups=mesh['grp'=2,'tgt'=4,'src'=4] {'src'}, dimensions={0}, use_global_device_ids=true | all-gather | bytes 737280 | tf_op jit(solution)/shard_map/all_gather | solution.py:21
  22.1 3.3 %convolution_convert_fusion = bf16[64,4,128]{2,0,1:T(8,128)(2,1)S(1)} fusion(bf16[4,4608,128]{2,1,0:T(8,128)(2,1)} %param.15, bf16[64,4608]{1,0:T(8,128)(2,1)S(1)} %all_gather.11), kind=kOutput, calls=%fused_computation.9 | convolution fusion | flops 302022656 | bytes 5373952 | tf_op jit(solution)/shard_map/sd,gde->sge/dot_general | solution.py:63
  25.4 1.0 collective-permute-start.3
  26.4 3.0 %collective-permute-start.5 = (bf16[64,512]{1,0:T(8,128)(2,1)S(1)}, bf16[64,512]{1,0:T(8,128)(2,1)S(1)}, u32[]{:S(2)}, u32[]{:S(2)}) collective-permute-start(bf16[64,512]{1,0:T(8,128)(2,1)S(1)} %copy_bitcast_fusion), channel_id=1, source_target_pairs={{0,12},{4,0},{8,4},{12,8},{1,13},{5,1},{9,5},{13,9},{2,14},{6,2},{... | collective-permute-start | bytes 196616 | tf_op jit(solution)/shard_map/while/body/eval_jaxpr/ppermute | solution.py:10
  29.4 53.4 %collective-permute-done.1 = bf16[8,1152,128]{2,1,0:T(8,128)(2,1)S(1)} collective-permute-done((bf16[8,1152,128]{2,1,0:T(8,128)(2,1)}, bf16[8,1152,128]{2,1,0:T(8,128)(2,1)S(1)}, u32[]{:S(2)}, u32[]{:S(2)}) %collective-permute-start.1) | collective-permute-done | bytes 2359328 | tf_op jit(solution)/shard_map/ppermute | solution.py:42
  82.8 49.3 %collective-permute-start.2 = (bf16[8,1152,128]{2,1,0:T(8,128)(2,1)S(1)}, bf16[8,1152,128]{2,1,0:T(8,128)(2,1)}, u32[]{:S(2)}, u32[]{:S(2)}) collective-permute-start(bf16[8,1152,128]{2,1,0:T(8,128)(2,1)S(1)} %collective-permute-done.1), channel_id=1, source_target_pairs={{0,4},{4,8},{8,12},{12,0},{1,5},{5,9},{9,13},{13,1},{2,6},{6,10},{... | collective-permute-start | bytes 7077896 | tf_op jit(solution)/shard_map/ppermute | solution.py:42
  132.1 0.7 compare_and_fusion
  137.2 0.8 collective-permute-done.3
  138.0 2.1 collective-permute-start.7
  140.7 1.8 collective-permute-start.6
  143.2 48.1 %collective-permute-done.7 = bf16[64,512]{1,0:T(8,128)(2,1)S(1)} collective-permute-done((bf16[64,512]{1,0:T(8,128)(2,1)S(1)}, bf16[64,512]{1,0:T(8,128)(2,1)S(1)}, u32[]{:S(2)}, u32[]{:S(2)}) %collective-permute-start.7) | collective-permute-done | bytes 65568 | tf_op jit(solution)/shard_map/ppermute | solution.py:10
  192.0 2.0 gather_fusion
  194.0 2.2 select_bitcast_fusion
  196.2 2.2 copy.27
  198.4 1.4 gather_fusion.4
  199.8 1.4 gather_fusion.3
  201.2 1.3 gather_fusion.2
  202.6 1.3 gather_fusion.1
  203.9 2.8 %fusion.13 = f32[256,8,128]{2,0,1:T(8,128)S(1)} fusion(bf16[8,1152,128]{2,1,0:T(8,128)(2,1)} %param.14, bf16[256,4608]{1,0:T(8,128)(2,1)} %all-gather.5.cloned.1.call-done, s32[]{:T(128)S(6)} %select_n.122), kind=kOutput, calls=%fused_computation.27 | convolution fusion | flops 603979776 | bytes 3997700 | tf_op jit(solution)/shard_map/td,hde->the/dot_general | solution.py:35
  206.7 2.5 convolution_add_fusion.2
  209.3 0.9 convolution_add_fusion.1
  210.2 2.6 %fusion = bf16[256,8,128]{2,0,1:T(8,128)(2,1)S(1)} fusion(f32[256,8,128]{2,0,1:T(8,128)S(1)} %convolution_add_fusion.1, bf16[8,1152,128]{2,1,0:T(8,128)(2,1)} %collective-permute-done.2, bf16[256,4608]{1,0:T(8,128)(2,1)S(1)} %copy-done, s32[]{:T(128)S(6)} %select_n.128), kind=kOutput, calls=%fused_computation.8 | convolution fusion | flops 604504064 | bytes 4521988 | tf_op jit(solution)/shard_map/td,hde->the/dot_general | solution.py:53
  215.0 1.6 fusion.8
  216.7 1.6 fusion.6
  218.8 1.6 fusion.4
  221.0 1.6 fusion.2
  222.6 0.7 copy-done.5
  223.4 22.4 %reduce-scatter.2.cloned.1.call-done = f32[64,256]{1,0:T(8,128)} async-done(((f32[256,256]{1,0:T(8,128)}), f32[64,256]{1,0:T(8,128)}) %reduce-scatter.2.cloned.1.call-update) | async-done | bytes 65552 | tf_op jit(solution)/shard_map/reduce_scatter | solution.py:114
  245.8 1.5 convert_element_type.69
  (78 shorter events, 7.1 us)
Async XLA Ops:
  6.5 185.4 %all-gather.3.cloned.1.call-start = ((), (), s32[]{:S(2)}) async-start(), calls=%async_computation.1 | async-start | bytes 1310720 | tf_op jit(solution)/shard_map/all_gather | solution.py:65
  8.4 195.5 %all-gather.5.cloned.1.call-start = ((), (), s32[]{:S(2)}) async-start(), calls=%async_computation.2 | async-start | bytes 2949120 | tf_op jit(solution)/shard_map/all_gather | solution.py:20
  8.5 74.3 %collective-permute-start.1 = (bf16[8,1152,128]{2,1,0:T(8,128)(2,1)}, bf16[8,1152,128]{2,1,0:T(8,128)(2,1)S(1)}, u32[]{:S(2)}, u32[]{:S(2)}) collective-permute-start(bf16[8,1152,128]{2,1,0:T(8,128)(2,1)} %param.14), channel_id=1, source_target_pairs={{0,4},{4,8},{8,12},{12,0},{1,5},{5,9},{9,13},{13,1},{2,6},{6,10},{... | collective-permute-start | bytes 7077896 | tf_op jit(solution)/shard_map/ppermute | solution.py:42
  11.6 234.2 %reduce-scatter.2.cloned.1.call-start = ((), (), s32[]{:S(2)}) async-start(), calls=%async_computation.3 | async-start | bytes 327680 | tf_op jit(solution)/shard_map/reduce_scatter | solution.py:114
  11.6 195.1 %collective-permute-start = (bf16[8,1152,128]{2,1,0:T(8,128)(2,1)}, bf16[8,1152,128]{2,1,0:T(8,128)(2,1)}, u32[]{:S(2)}, u32[]{:S(2)}) collective-permute-start(bf16[8,1152,128]{2,1,0:T(8,128)(2,1)} %param.14), channel_id=1, source_target_pairs={{0,12},{4,0},{8,4},{12,8},{1,13},{5,1},{9,5},{13,9},{2,14},{6,2},{... | collective-permute-start | bytes 7077896 | tf_op jit(solution)/shard_map/ppermute | solution.py:44
  14.3 177.6 %collective-permute-start.4 = (bf16[16,4608]{1,0:T(8,128)(2,1)}, bf16[16,4608]{1,0:T(8,128)(2,1)}, u32[]{:S(2)}, u32[]{:S(2)}) collective-permute-start(bf16[16,4608]{1,0:T(8,128)(2,1)} %param.12), channel_id=1, source_target_pairs={{0,4},{4,8},{8,12},{12,0},{1,5},{5,9},{9,13},{13,1},{2,6},{6,10},{... | collective-permute-start | bytes 442376 | tf_op jit(solution)/shard_map/while/body/eval_jaxpr/ppermute | solution.py:10
  22.1 110.0 %copy-start.8 = (s32[256]{0:T(256)S(1)}, s32[256]{0:T(256)}, u32[]{:S(2)}) copy-start(s32[256]{0:T(256)} %param.11) | copy-start | bytes 3076
  22.1 110.0 %copy-start.9 = (s32[256]{0:T(256)S(1)}, s32[256]{0:T(256)}, u32[]{:S(2)}) copy-start(s32[256]{0:T(256)} %param.13) | copy-start | bytes 3076
  22.1 111.8 %copy-start.14 = (s32[4,4]{1,0:T(4,128)S(1)}, s32[4,4]{1,0:T(4,128)}, u32[]{:S(2)}) copy-start(s32[4,4]{1,0:T(4,128)} %param.17) | copy-start | bytes 196
  25.4 112.6 %collective-permute-start.3 = (bf16[64,512]{1,0:T(8,128)(2,1)S(1)}, bf16[64,512]{1,0:T(8,128)(2,1)S(1)}, u32[]{:S(2)}, u32[]{:S(2)}) collective-permute-start(bf16[64,512]{1,0:T(8,128)(2,1)S(1)} %copy_bitcast_fusion), channel_id=1, source_target_pairs={{0,4},{4,8},{8,12},{12,0},{1,5},{5,9},{9,13},{13,1},{2,6},{6,10},{... | collective-permute-start | bytes 196616 | tf_op jit(solution)/shard_map/while/body/eval_jaxpr/ppermute | solution.py:10
  26.4 114.3 %collective-permute-start.5 = (bf16[64,512]{1,0:T(8,128)(2,1)S(1)}, bf16[64,512]{1,0:T(8,128)(2,1)S(1)}, u32[]{:S(2)}, u32[]{:S(2)}) collective-permute-start(bf16[64,512]{1,0:T(8,128)(2,1)S(1)} %copy_bitcast_fusion), channel_id=1, source_target_pairs={{0,12},{4,0},{8,4},{12,8},{1,13},{5,1},{9,5},{13,9},{2,14},{6,2},{... | collective-permute-start | bytes 196616 | tf_op jit(solution)/shard_map/while/body/eval_jaxpr/ppermute | solution.py:10
  82.8 127.4 %collective-permute-start.2 = (bf16[8,1152,128]{2,1,0:T(8,128)(2,1)S(1)}, bf16[8,1152,128]{2,1,0:T(8,128)(2,1)}, u32[]{:S(2)}, u32[]{:S(2)}) collective-permute-start(bf16[8,1152,128]{2,1,0:T(8,128)(2,1)S(1)} %collective-permute-done.1), channel_id=1, source_target_pairs={{0,4},{4,8},{8,12},{12,0},{1,5},{5,9},{9,13},{13,1},{2,6},{6,10},{... | collective-permute-start | bytes 7077896 | tf_op jit(solution)/shard_map/ppermute | solution.py:42
  138.0 53.4 %collective-permute-start.7 = (bf16[64,512]{1,0:T(8,128)(2,1)S(1)}, bf16[64,512]{1,0:T(8,128)(2,1)S(1)}, u32[]{:S(2)}, u32[]{:S(2)}) collective-permute-start(bf16[64,512]{1,0:T(8,128)(2,1)S(1)} %collective-permute-done.3), channel_id=1, source_target_pairs={{0,4},{4,8},{8,12},{12,0},{1,5},{5,9},{9,13},{13,1},{2,6},{6,10},{... | collective-permute-start | bytes 196616 | tf_op jit(solution)/shard_map/ppermute | solution.py:10
  140.7 78.1 %collective-permute-start.6 = (bf16[16,4608]{1,0:T(8,128)(2,1)}, bf16[16,4608]{1,0:T(8,128)(2,1)}, u32[]{:S(2)}, u32[]{:S(2)}) collective-permute-start(bf16[16,4608]{1,0:T(8,128)(2,1)} %param.12), channel_id=1, source_target_pairs={{0,12},{4,0},{8,4},{12,8},{1,13},{5,1},{9,5},{13,9},{2,14},{6,2},{... | collective-permute-start | bytes 442376 | tf_op jit(solution)/shard_map/while/body/eval_jaxpr/ppermute | solution.py:10
  192.0 29.0 %collective-permute-start.8 = (bf16[16,4608]{1,0:T(8,128)(2,1)}, bf16[16,4608]{1,0:T(8,128)(2,1)}, u32[]{:S(2)}, u32[]{:S(2)}) collective-permute-start(bf16[16,4608]{1,0:T(8,128)(2,1)} %collective-permute-done.4), channel_id=1, source_target_pairs={{0,4},{4,8},{8,12},{12,0},{1,5},{5,9},{9,13},{13,1},{2,6},{6,10},{... | collective-permute-start | bytes 442376 | tf_op jit(solution)/shard_map/ppermute | solution.py:10
  203.9 2.9 %copy-start = (bf16[256,4608]{1,0:T(8,128)(2,1)S(1)}, bf16[256,4608]{1,0:T(8,128)(2,1)}, u32[]{:S(2)}) copy-start(bf16[256,4608]{1,0:T(8,128)(2,1)} %all-gather.5.cloned.1.call-done) | copy-start | bytes 7077892
  210.1 2.9 %copy-start.7 = (bf16[64,4,128]{2,1,0:T(4,128)(2,1)S(1)}, bf16[64,4,128]{2,1,0:T(4,128)(2,1)}, u32[]{:S(2)}) copy-start(bf16[64,4,128]{2,1,0:T(4,128)(2,1)} %reshape.57) | copy-start | bytes 196612
  210.1 3.3 %copy-start.6 = (bf16[64,4,128]{2,1,0:T(4,128)(2,1)S(1)}, bf16[64,4,128]{2,1,0:T(4,128)(2,1)}, u32[]{:S(2)}) copy-start(bf16[64,4,128]{2,1,0:T(4,128)(2,1)} %reshape.55) | copy-start | bytes 196612
  212.7 1.3 copy-start.4
  212.7 1.3 copy-start.13
  213.1 1.4 copy-start.3
  213.1 1.4 copy-start.12
  213.1 1.9 copy-start.18
  214.0 2.7 %copy-start.17 = (s32[16]{0:T(128)S(1)}, s32[16]{0:T(128)}, u32[]{:S(2)}) copy-start(s32[16]{0:T(128)} %get-tuple-element.65) | copy-start | bytes 196
  214.9 3.4 %copy-start.2 = (bf16[64,8,256]{2,1,0:T(8,128)(2,1)S(1)}, bf16[64,8,256]{2,1,0:T(8,128)(2,1)}, u32[]{:S(2)}) copy-start(bf16[64,8,256]{2,1,0:T(8,128)(2,1)} %gather_fusion.3) | copy-start | bytes 786436
  214.9 3.4 %copy-start.11 = (pred[64]{0:T(512)(128)(4,1)S(1)}, pred[64]{0:T(512)(128)(4,1)}, u32[]{:S(2)}) copy-start(pred[64]{0:T(512)(128)(4,1)} %get-tuple-element.67) | copy-start | bytes 196
  216.6 2.2 copy-start.16
  218.3 2.2 copy-start.1
  218.3 2.2 copy-start.10
  218.3 2.6 %copy-start.15 = (s32[16]{0:T(128)S(1)}, s32[16]{0:T(128)}, u32[]{:S(2)}) copy-start(s32[16]{0:T(128)} %get-tuple-element.62) | copy-start | bytes 196
  222.6 0.7 copy-start.5
Sparse Core Ops, SparseCore 0:
  8.9 81.8 all-gather.2
  92.3 22.7 all-gather.4
  223.5 22.2 reduce-scatter.1
